TPU v7x, 32 devices: a whole 2x2x4 slice. The times are simulated.
32 devices in a mesh: sa: 4 (over y, core), sb: 8 (over z, x).
Axes of the slice: x: 2, y: 2, z: 4, core: 2. Of those that a mesh axis runs over, the one named last changes fastest.
Arguments:
- queries: bfloat16 [1024, 1024], P(('sa', 'sb')), may hold values from -6 to 6
- out_grad: bfloat16 [1024, 1024], P(('sa', 'sb')), may hold values from -6144 to 6144
- forward_out: bfloat16 [1024, 1024], P(('sa', 'sb')), may hold values from -3 to 3
- lse_shift: float32 [1024, 8], P(('sa', 'sb')), may hold values from 0.2 to 1
- key_rows: bfloat16 [32768, 256], P(('sa', 'sb')), may hold values from -7 to 7
- value_rows: bfloat16 [32768, 256], P(('sa', 'sb')), may hold values from -6 to 6
Outputs:
- query_grad: float32 [1024, 1024], P(('sa', 'sb'))
- key_grad: bfloat16 [32768, 256], P(('sa', 'sb'))
- value_grad: bfloat16 [32768, 256], P(('sa', 'sb'))
All inputs are finite; a program needn't handle non-finite values.
Results may differ from a plain program's by a relative error of at most 0.0097.
Values may be sent and summed in bfloat16 or wider, within the bound.
A program may use at most 64 MiB of HBM per device.

v0:
```python
import math
import jax
import jax.numpy as jnp
from jax import lax
from jax.sharding import PartitionSpec as P

QH = 8
KVH = 2
HEAD_DIM = 128


def head_delta(grad_part, output_part):
    product = grad_part.astype(jnp.float32) * output_part.astype(jnp.float32)
    return jnp.sum(product.reshape(product.shape[0], QH, HEAD_DIM), axis=-1)


def local(queries, out_grad, forward_out, lse_shift, key_rows, value_rows):
    per_group = QH // KVH
    score_scale = 1.0 / math.sqrt(HEAD_DIM)
    devices = lax.axis_size("sa") * lax.axis_size("sb")
    local_keys = key_rows.shape[0]
    total_keys = local_keys * devices
    key_total = lax.psum(jnp.sum(key_rows.astype(jnp.float32), axis=0), ("sa", "sb"))
    smoothed = (key_rows.astype(jnp.float32) - key_total / total_keys).astype(jnp.bfloat16)
    query_all, grad_all, output_all = (
        lax.all_gather(queries, ("sa", "sb"), axis=0, tiled=True),
        lax.all_gather(out_grad, ("sa", "sb"), axis=0, tiled=True),
        lax.all_gather(forward_out, ("sa", "sb"), axis=0, tiled=True),
    )
    shift_all = lax.all_gather(lse_shift, ("sa", "sb"), axis=0, tiled=True)
    delta_all = head_delta(grad_all, output_all)
    offset_all = shift_all + math.log(total_keys)

    def one_head(head):
        shared = head // per_group
        head_queries = lax.dynamic_slice_in_dim(query_all, head * HEAD_DIM, HEAD_DIM, 1)
        head_grads = lax.dynamic_slice_in_dim(grad_all, head * HEAD_DIM, HEAD_DIM, 1)
        head_keys = lax.dynamic_slice_in_dim(smoothed, shared * HEAD_DIM, HEAD_DIM, 1)
        head_values = lax.dynamic_slice_in_dim(value_rows, shared * HEAD_DIM, HEAD_DIM, 1)
        head_offset = lax.dynamic_slice_in_dim(offset_all, head, 1, 1)
        head_deltas = lax.dynamic_slice_in_dim(delta_all, head, 1, 1)
        scores = (
            jnp.einsum("qd,kd->qk", head_queries, head_keys, preferred_element_type=jnp.float32)
            * score_scale
        )
        prob = jnp.exp(scores - head_offset)
        prob_low = prob.astype(jnp.bfloat16)
        value_part = jnp.einsum(
            "qk,qd->kd", prob_low, head_grads, preferred_element_type=jnp.float32
        )
        dprob = jnp.einsum("qd,kd->qk", head_grads, head_values, preferred_element_type=jnp.float32)
        dscore = (prob * (dprob - head_deltas)).astype(jnp.bfloat16)
        key_part = (
            jnp.einsum("qk,qd->kd", dscore, head_queries, preferred_element_type=jnp.float32)
            * score_scale
        )
        query_part = (
            jnp.einsum("qk,kd->qd", dscore, head_keys, preferred_element_type=jnp.float32)
            * score_scale
        )
        return (query_part, key_part, value_part)

    query_heads, key_heads, value_heads = lax.map(one_head, jnp.arange(QH, dtype=jnp.int32))
    key_sum = key_heads.reshape(KVH, per_group, local_keys, HEAD_DIM).sum(axis=1)
    value_sum = value_heads.reshape(KVH, per_group, local_keys, HEAD_DIM).sum(axis=1)
    key_grad = key_sum.transpose(1, 0, 2).reshape(local_keys, KVH * HEAD_DIM).astype(jnp.bfloat16)
    value_grad = (
        value_sum.transpose(1, 0, 2).reshape(local_keys, KVH * HEAD_DIM).astype(jnp.bfloat16)
    )
    halfway = lax.psum_scatter(
        query_heads.astype(jnp.bfloat16), "sa", scatter_dimension=1, tiled=True
    )
    owned = lax.psum_scatter(halfway, "sb", scatter_dimension=1, tiled=True).astype(jnp.float32)
    query_grad = owned.transpose(1, 0, 2).reshape(owned.shape[1], QH * HEAD_DIM)
    return (query_grad, key_grad, value_grad)


def solution(mesh):
    in_specs = (
        P(("sa", "sb"), None),
        P(("sa", "sb"), None),
        P(("sa", "sb"), None),
        P(("sa", "sb"), None),
        P(("sa", "sb"), None),
        P(("sa", "sb"), None),
    )
    out_specs = (P(("sa", "sb"), None), P(("sa", "sb"), None), P(("sa", "sb"), None))
    return jax.shard_map(local, mesh=mesh, in_specs=in_specs, out_specs=out_specs, check_vma=False)
```

profile of v0, /device:TPU:0, one launch (start us, length us, event | category | flops | bytes accessed | tf_op | source)
XLA Modules:
  0.0 444.5 jit_solution(709339691636741124)
XLA Ops:
  9.5 70.8 %all-gather = f32[32,32,8]{1,2,0:T(8,128)S(1)} all-gather(f32[1,32,8]{1,2,0:T(8,128)} %bitcast.65), channel_id=1, replica_groups=mesh['sa'=4,'sb'=8] {'sa','sb'}, dimensions={0}, use_global_device_ids=true | all-gather | bytes 33792 | tf_op jit(solution)/shard_map/all_gather | solution.py:30
  81.6 37.2 %psum.7 = f32[256]{0:T(256)S(1)} all-reduce(f32[256]{0:T(256)S(1)} %convert_reduce_fusion), channel_id=1, replica_groups=mesh['sa'=4,'sb'=8] {'sa','sb'}, use_global_device_ids=true, to_apply=%region_1.0 | all-reduce | flops 256 | bytes 2048 | tf_op jit(solution)/shard_map/psum | solution.py:23
  120.0 9.0 %all-gather.9.cloned.1.call-done = bf16[1024,1024]{1,0:T(8,128)(2,1)} async-done(((bf16[32,1024]{1,0:T(8,128)(2,1)}), bf16[1024,1024]{1,0:T(8,128)(2,1)}) %all-gather.9.cloned.1.call-update) | async-done | bytes 2097168 | tf_op jit(solution)/shard_map/all_gather | solution.py:28
  128.9 3.1 multiply_bitcast_fusion
  132.1 3.0 copy.21
  135.0 3.4 reduce_sum.37
  138.6 48.5 %all-gather.5.cloned.1.call-done = bf16[1024,1024]{1,0:T(8,128)(2,1)} async-done(((bf16[32,1024]{1,0:T(8,128)(2,1)}), bf16[1024,1024]{1,0:T(8,128)(2,1)}) %all-gather.5.cloned.1.call-update) | async-done | bytes 2097168 | tf_op jit(solution)/shard_map/all_gather | solution.py:26
  187.2 152.8 %while.16 = (s32[]{:T(128)}, bf16[8,1024,128]{2,1,0:T(8,128)(2,1)}, f32[8,1024,128]{2,1,0:T(8,128)}, f32[8,1024,128]{2,1,0:T(8,128)}, s32[8]{0:T(128)S(1)}, /*in...) while((s32[]{:T(128)}, bf16[8,1024,128]{2,1,0:T(8,128)(2,1)}, ...), condition=%wide.region_4.5_spmd, body=%wide.region_3.4_spmd.sunk | while | flops 1350828032 | bytes 39090184 | solution.py:63
  191.0 3.6 fusion.56
  196.0 3.5 multiply_convert_fusion.2
  199.4 2.5 fusion.58
  201.9 2.9 fusion.59
  210.1 3.6 fusion.56
  215.0 3.5 multiply_convert_fusion.2
  218.5 2.5 fusion.58
  221.0 2.9 fusion.59
  229.2 3.6 fusion.56
  234.1 3.5 multiply_convert_fusion.2
  237.6 2.5 fusion.58
  240.1 2.9 fusion.59
  248.3 3.6 fusion.56
  253.2 3.5 multiply_convert_fusion.2
  256.7 2.5 fusion.58
  259.2 2.9 fusion.59
  267.4 3.6 fusion.56
  272.4 3.5 multiply_convert_fusion.2
  275.8 2.5 fusion.58
  278.3 2.9 fusion.59
  281.2 1.4 fusion.57
  286.5 3.6 fusion.56
  291.5 3.5 multiply_convert_fusion.2
  294.9 2.5 fusion.58
  297.5 2.9 fusion.59
  300.4 1.4 fusion.57
  305.6 3.6 fusion.56
  310.6 3.5 multiply_convert_fusion.2
  314.1 2.5 fusion.58
  316.6 2.9 fusion.59
  319.4 1.4 fusion.57
  324.7 3.6 fusion.56
  329.7 3.5 multiply_convert_fusion.2
  333.2 2.5 fusion.58
  335.7 2.9 fusion.59
  338.6 1.4 fusion.57
  340.1 30.1 %reduce-scatter.3.cloned.1.call-done = bf16[8,256,128]{2,1,0:T(8,128)(2,1)} async-done(((bf16[8,1024,128]{2,1,0:T(8,128)(2,1)}), bf16[8,256,128]{2,1,0:T(8,128)(2,1)}) %reduce-scatter.3.cloned.1.call-update) | async-done | bytes 524304 | tf_op jit(solution)/shard_map/reduce_scatter | solution.py:70
  370.2 4.3 bitcast_reduce_fusion
  377.0 59.4 %reduce-scatter.5.cloned.1.call-done = bf16[8,32,128]{2,1,0:T(8,128)(2,1)} async-done(((bf16[8,256,128]{2,1,0:T(8,128)(2,1)}), bf16[8,32,128]{2,1,0:T(8,128)(2,1)}) %reduce-scatter.5.cloned.1.call-update) | async-done | bytes 65552 | tf_op jit(solution)/shard_map/reduce_scatter | solution.py:73
  436.4 1.5 copy_bitcast_fusion
  (64 shorter events, 17.8 us)
Async XLA Ops:
  7.2 112.8 %all-gather.7.cloned.1.call-start = ((), (), s32[]{:S(2)}) async-start(), calls=%async_computation.3 | async-start | bytes 2162688 | tf_op jit(solution)/shard_map/all_gather | solution.py:27
  7.9 121.0 %all-gather.9.cloned.1.call-start = ((), (), s32[]{:S(2)}) async-start(), calls=%async_computation.4 | async-start | bytes 2162688 | tf_op jit(solution)/shard_map/all_gather | solution.py:28
  8.6 178.5 %all-gather.5.cloned.1.call-start = ((), (), s32[]{:S(2)}) async-start(), calls=%async_computation.2 | async-start | bytes 2162688 | tf_op jit(solution)/shard_map/all_gather | solution.py:26
  9.4 360.8 %reduce-scatter.3.cloned.1.call-start = ((), (), s32[]{:S(2)}) async-start(), calls=%async_computation.5 | async-start | bytes 2621440 | tf_op jit(solution)/shard_map/reduce_scatter | solution.py:70
  135.0 52.1 %copy-start.1 = (bf16[1024,256]{1,0:T(8,128)(2,1)S(1)}, bf16[1024,256]{1,0:T(8,128)(2,1)}, u32[]{:S(2)}) copy-start(bf16[1024,256]{1,0:T(8,128)(2,1)} %param.13) | copy-start | bytes 1572868
  196.0 6.0 %copy-start = (f32[1024,1024]{1,0:T(8,128)S(1)}, f32[1024,1024]{1,0:T(8,128)}, u32[]{:S(2)}) copy-start(f32[1024,1024]{1,0:T(8,128)} %fusion.56) | copy-start | bytes 12582916 | tf_op jit(solution)/shard_map/while
  215.0 6.0 %copy-start = (f32[1024,1024]{1,0:T(8,128)S(1)}, f32[1024,1024]{1,0:T(8,128)}, u32[]{:S(2)}) copy-start(f32[1024,1024]{1,0:T(8,128)} %fusion.56) | copy-start | bytes 12582916 | tf_op jit(solution)/shard_map/while
  234.1 6.0 %copy-start = (f32[1024,1024]{1,0:T(8,128)S(1)}, f32[1024,1024]{1,0:T(8,128)}, u32[]{:S(2)}) copy-start(f32[1024,1024]{1,0:T(8,128)} %fusion.56) | copy-start | bytes 12582916 | tf_op jit(solution)/shard_map/while
  253.2 6.0 %copy-start = (f32[1024,1024]{1,0:T(8,128)S(1)}, f32[1024,1024]{1,0:T(8,128)}, u32[]{:S(2)}) copy-start(f32[1024,1024]{1,0:T(8,128)} %fusion.56) | copy-start | bytes 12582916 | tf_op jit(solution)/shard_map/while
  272.4 6.0 %copy-start = (f32[1024,1024]{1,0:T(8,128)S(1)}, f32[1024,1024]{1,0:T(8,128)}, u32[]{:S(2)}) copy-start(f32[1024,1024]{1,0:T(8,128)} %fusion.56) | copy-start | bytes 12582916 | tf_op jit(solution)/shard_map/while
  291.5 6.0 %copy-start = (f32[1024,1024]{1,0:T(8,128)S(1)}, f32[1024,1024]{1,0:T(8,128)}, u32[]{:S(2)}) copy-start(f32[1024,1024]{1,0:T(8,128)} %fusion.56) | copy-start | bytes 12582916 | tf_op jit(solution)/shard_map/while
  310.6 6.0 %copy-start = (f32[1024,1024]{1,0:T(8,128)S(1)}, f32[1024,1024]{1,0:T(8,128)}, u32[]{:S(2)}) copy-start(f32[1024,1024]{1,0:T(8,128)} %fusion.56) | copy-start | bytes 12582916 | tf_op jit(solution)/shard_map/while
  329.7 6.0 %copy-start = (f32[1024,1024]{1,0:T(8,128)S(1)}, f32[1024,1024]{1,0:T(8,128)}, u32[]{:S(2)}) copy-start(f32[1024,1024]{1,0:T(8,128)} %fusion.56) | copy-start | bytes 12582916 | tf_op jit(solution)/shard_map/while
  340.0 96.4 %reduce-scatter.5.cloned.1.call-start = ((), (), s32[]{:S(2)}) async-start(), calls=%async_computation.6 | async-start | bytes 589824 | tf_op jit(solution)/shard_map/reduce_scatter | solution.py:73
Sparse Core Ops, SparseCore 0:
  11.0 59.4 all-gather.6
  73.4 55.4 all-gather.8
  131.9 55.1 all-gather.4
  340.1 30.0 reduce-scatter.2
  373.4 63.0 reduce-scatter.4
where the time goes:
time: 446 us; the launch traced here: 444 us
  waiting for transfers between devices  149 us (33%)
  matrix products  111 us (25%)
  blocking collectives  108 us (24%)
  loops' own time  36.7 us (8%)
  other arithmetic  14.7 us (3%)
  between operations  13.9 us (3%)
  local copies, waits for them, and re-layouts  10.5 us (2%)
    all_gather x1, blocking collectives, local(): shift_all = lax.all_gather(lse_shift, ('sa', 'sb'), axis=0, tiled=True)  70.8 us
    reduce_scatter x1, waiting for transfers between devices, local(): lax.psum_scatter(halfway, 'sb', scatter_dimension=1, tiled=True)  59.4 us
    all_gather x1, waiting for transfers between devices, local(): lax.all_gather(queries, ('sa', 'sb'), axis=0, tiled=True)  48.5 us
    psum x1, blocking collectives, local(): lax.psum(jnp.sum(key_rows.astype(jnp.float32), axis=0), ('sa', 'sb'))  37.2 us
    another operation x1, loops' own time, local(): lax.map(one_head, jnp.arange(QH, dtype=jnp.int32))  36.7 us
    reduce_scatter x1, waiting for transfers between devices, local(): lax.psum_scatter(query_heads.astype(jnp.bfloat16), 'sa', scatter_dimensio...  30.1 us
    dot_general x8, matrix products, one_head(): jnp.einsum('qd,kd->qk', head_queries, head_keys, preferred_element_type=j...  29.1 us
    dot_general x8, matrix products, one_head(): jnp.einsum('qd,kd->qk', head_grads, head_values, preferred_element_type=j...  27.7 us
  transfers between devices with their start and end apart: 5, of which 4 were waited for; matrix products, arithmetic and copies ran while one was open for 4% of the time, Pallas kernels for 0%

commit v1 on v0

--- a/solution.py
+++ b/solution.py
@@ -20,7 +20,9 @@
     devices = lax.axis_size("sa") * lax.axis_size("sb")
     local_keys = key_rows.shape[0]
     total_keys = local_keys * devices
-    key_total = lax.psum(jnp.sum(key_rows.astype(jnp.float32), axis=0), ("sa", "sb"))
+    key_total = jnp.sum(
+        lax.all_gather(jnp.sum(key_rows.astype(jnp.float32), axis=0), ("sa", "sb")), axis=0
+    )
     smoothed = (key_rows.astype(jnp.float32) - key_total / total_keys).astype(jnp.bfloat16)
     query_all, grad_all, output_all = (
         lax.all_gather(queries, ("sa", "sb"), axis=0, tiled=True),

time: 446 us -> 446 us (level)
  blocking collectives: 108 us -> 134 us
  waiting for transfers between devices: 149 us -> 123 us
    all_gather x0 -> x1, blocking collectives: none -> 63.6 us  [local(): lax.all_gather(jnp.sum(key_rows.astype(jnp.float32), axis=0), ('sa', 'sb'))]
    psum x1 -> x0, blocking collectives: 37.2 us -> none  [local(): lax.psum(jnp.sum(key_rows.astype(jnp.float32), axis=0), ('sa', 'sb'))]
    all_gather x1, waiting for transfers between devices: 48.5 us -> 30.8 us  [local(): lax.all_gather(queries, ('sa', 'sb'), axis=0, tiled=True)]
    all_gather x1, waiting for transfers between devices: 8.96 us -> 0.02 us  [local(): lax.all_gather(forward_out, ('sa', 'sb'), axis=0, tiled=True)]
  transfers between devices with their start and end apart: 5 -> 5, of which waited for: 4 -> 3; matrix products, arithmetic and copies ran while one was open for 4% -> 4% of each run, Pallas kernels for 0% -> 0%
where the time goes in v1:
time: 446 us; the launch traced here: 444 us
  blocking collectives  134 us (30%)
  waiting for transfers between devices  123 us (28%)
  matrix products  111 us (25%)
  loops' own time  36.7 us (8%)
  other arithmetic  14.8 us (3%)
  between operations  13.9 us (3%)
  local copies, waits for them, and re-layouts  10.5 us (2%)
    all_gather x1, blocking collectives, local(): shift_all = lax.all_gather(lse_shift, ('sa', 'sb'), axis=0, tiled=True)  70.8 us
    all_gather x1, blocking collectives, local(): lax.all_gather(jnp.sum(key_rows.astype(jnp.float32), axis=0), ('sa', 'sb'))  63.6 us
    reduce_scatter x1, waiting for transfers between devices, local(): lax.psum_scatter(halfway, 'sb', scatter_dimension=1, tiled=True)  59.4 us
    another operation x1, loops' own time, local(): lax.map(one_head, jnp.arange(QH, dtype=jnp.int32))  36.7 us
    all_gather x1, waiting for transfers between devices, local(): lax.all_gather(queries, ('sa', 'sb'), axis=0, tiled=True)  30.8 us
    reduce_scatter x1, waiting for transfers between devices, local(): lax.psum_scatter(query_heads.astype(jnp.bfloat16), 'sa', scatter_dimensio...  30.1 us
    dot_general x8, matrix products, one_head(): jnp.einsum('qd,kd->qk', head_queries, head_keys, preferred_element_type=j...  29.1 us
    dot_general x8, matrix products, one_head(): jnp.einsum('qd,kd->qk', head_grads, head_values, preferred_element_type=j...  27.7 us
  transfers between devices with their start and end apart: 5, of which 3 were waited for; matrix products, arithmetic and copies ran while one was open for 4% of the time, Pallas kernels for 0%

profile of v1, /device:TPU:0, one launch (start us, length us, event | category | flops | bytes accessed | tf_op | source)
XLA Modules:
  0.0 444.3 jit_solution(3396659285432956975)
XLA Ops:
  9.5 70.8 %all-gather.2 = f32[32,32,8]{1,2,0:T(8,128)S(1)} all-gather(f32[1,32,8]{1,2,0:T(8,128)} %bitcast.67), channel_id=1, replica_groups=mesh['sa'=4,'sb'=8] {'sa','sb'}, dimensions={0}, use_global_device_ids=true | all-gather | bytes 33792 | tf_op jit(solution)/shard_map/all_gather | solution.py:32
  81.6 63.6 %all-gather.1 = f32[32,1,256]{2,1,0:T(1,128)S(1)} all-gather(f32[1,1,256]{2,1,0:T(1,128)S(1)} %bitcast.66), channel_id=2, replica_groups=mesh['sa'=4,'sb'=8] {'sa','sb'}, dimensions={0}, use_global_device_ids=true | all-gather | bytes 33792 | tf_op jit(solution)/shard_map/all_gather | solution.py:24
  146.5 3.1 multiply_bitcast_fusion
  149.6 3.0 copy.21
  152.6 3.4 reduce_sum.47
  156.2 30.8 %all-gather.7.cloned.1.call-done = bf16[1024,1024]{1,0:T(8,128)(2,1)} async-done(((bf16[32,1024]{1,0:T(8,128)(2,1)}), bf16[1024,1024]{1,0:T(8,128)(2,1)}) %all-gather.7.cloned.1.call-update) | async-done | bytes 2097168 | tf_op jit(solution)/shard_map/all_gather | solution.py:28
  187.0 152.8 %while.16 = (s32[]{:T(128)}, bf16[8,1024,128]{2,1,0:T(8,128)(2,1)}, f32[8,1024,128]{2,1,0:T(8,128)}, f32[8,1024,128]{2,1,0:T(8,128)}, s32[8]{0:T(128)S(1)}, /*in...) while((s32[]{:T(128)}, bf16[8,1024,128]{2,1,0:T(8,128)(2,1)}, ...), condition=%wide.region_4.5_spmd, body=%wide.region_3.4_spmd.sunk | while | flops 1350828032 | bytes 39090184 | solution.py:65
  190.8 3.6 fusion.56
  195.8 3.5 multiply_convert_fusion.2
  199.3 2.5 fusion.58
  201.8 2.9 fusion.59
  209.9 3.6 fusion.56
  214.8 3.5 multiply_convert_fusion.2
  218.3 2.5 fusion.58
  220.8 2.9 fusion.59
  229.0 3.6 fusion.56
  233.9 3.5 multiply_convert_fusion.2
  237.4 2.5 fusion.58
  239.9 2.9 fusion.59
  248.1 3.6 fusion.56
  253.1 3.5 multiply_convert_fusion.2
  256.5 2.5 fusion.58
  259.1 2.9 fusion.59
  261.9 1.4 fusion.57
  267.2 3.6 fusion.56
  272.2 3.5 multiply_convert_fusion.2
  275.6 2.5 fusion.58
  278.1 2.9 fusion.59
  281.0 1.4 fusion.57
  286.3 3.6 fusion.56
  291.3 3.5 multiply_convert_fusion.2
  294.8 2.5 fusion.58
  297.3 2.9 fusion.59
  300.2 1.4 fusion.57
  305.5 3.6 fusion.56
  310.4 3.5 multiply_convert_fusion.2
  313.9 2.5 fusion.58
  316.4 2.9 fusion.59
  319.2 1.4 fusion.57
  324.5 3.6 fusion.56
  329.5 3.5 multiply_convert_fusion.2
  333.0 2.5 fusion.58
  335.5 2.9 fusion.59
  338.4 1.4 fusion.57
  339.9 30.1 %reduce-scatter.3.cloned.1.call-done = bf16[8,256,128]{2,1,0:T(8,128)(2,1)} async-done(((bf16[8,1024,128]{2,1,0:T(8,128)(2,1)}), bf16[8,256,128]{2,1,0:T(8,128)(2,1)}) %reduce-scatter.3.cloned.1.call-update) | async-done | bytes 524304 | tf_op jit(solution)/shard_map/reduce_scatter | solution.py:72
  370.0 4.3 bitcast_reduce_fusion
  376.8 59.4 %reduce-scatter.5.cloned.1.call-done = bf16[8,32,128]{2,1,0:T(8,128)(2,1)} async-done(((bf16[8,256,128]{2,1,0:T(8,128)(2,1)}), bf16[8,32,128]{2,1,0:T(8,128)(2,1)}) %reduce-scatter.5.cloned.1.call-update) | async-done | bytes 65552 | tf_op jit(solution)/shard_map/reduce_scatter | solution.py:75
  436.2 1.5 copy_bitcast_fusion
  (65 shorter events, 16.5 us)
Async XLA Ops:
  7.2 139.3 %all-gather.9.cloned.1.call-start = ((), (), s32[]{:S(2)}) async-start(), calls=%async_computation.3 | async-start | bytes 2162688 | tf_op jit(solution)/shard_map/all_gather | solution.py:29
  7.9 138.5 %all-gather.11.cloned.1.call-start = ((), (), s32[]{:S(2)}) async-start(), calls=%async_computation.4 | async-start | bytes 2162688 | tf_op jit(solution)/shard_map/all_gather | solution.py:30
  8.6 178.3 %all-gather.7.cloned.1.call-start = ((), (), s32[]{:S(2)}) async-start(), calls=%async_computation.2 | async-start | bytes 2162688 | tf_op jit(solution)/shard_map/all_gather | solution.py:28
  9.4 360.6 %reduce-scatter.3.cloned.1.call-start = ((), (), s32[]{:S(2)}) async-start(), calls=%async_computation.5 | async-start | bytes 2621440 | tf_op jit(solution)/shard_map/reduce_scatter | solution.py:72
  152.6 34.4 %copy-start.1 = (bf16[1024,256]{1,0:T(8,128)(2,1)S(1)}, bf16[1024,256]{1,0:T(8,128)(2,1)}, u32[]{:S(2)}) copy-start(bf16[1024,256]{1,0:T(8,128)(2,1)} %param.13) | copy-start | bytes 1572868
  195.8 6.0 %copy-start = (f32[1024,1024]{1,0:T(8,128)S(1)}, f32[1024,1024]{1,0:T(8,128)}, u32[]{:S(2)}) copy-start(f32[1024,1024]{1,0:T(8,128)} %fusion.56) | copy-start | bytes 12582916 | tf_op jit(solution)/shard_map/while
  214.8 6.0 %copy-start = (f32[1024,1024]{1,0:T(8,128)S(1)}, f32[1024,1024]{1,0:T(8,128)}, u32[]{:S(2)}) copy-start(f32[1024,1024]{1,0:T(8,128)} %fusion.56) | copy-start | bytes 12582916 | tf_op jit(solution)/shard_map/while
  233.9 6.0 %copy-start = (f32[1024,1024]{1,0:T(8,128)S(1)}, f32[1024,1024]{1,0:T(8,128)}, u32[]{:S(2)}) copy-start(f32[1024,1024]{1,0:T(8,128)} %fusion.56) | copy-start | bytes 12582916 | tf_op jit(solution)/shard_map/while
  253.0 6.0 %copy-start = (f32[1024,1024]{1,0:T(8,128)S(1)}, f32[1024,1024]{1,0:T(8,128)}, u32[]{:S(2)}) copy-start(f32[1024,1024]{1,0:T(8,128)} %fusion.56) | copy-start | bytes 12582916 | tf_op jit(solution)/shard_map/while
  272.2 6.0 %copy-start = (f32[1024,1024]{1,0:T(8,128)S(1)}, f32[1024,1024]{1,0:T(8,128)}, u32[]{:S(2)}) copy-start(f32[1024,1024]{1,0:T(8,128)} %fusion.56) | copy-start | bytes 12582916 | tf_op jit(solution)/shard_map/while
  291.3 6.0 %copy-start = (f32[1024,1024]{1,0:T(8,128)S(1)}, f32[1024,1024]{1,0:T(8,128)}, u32[]{:S(2)}) copy-start(f32[1024,1024]{1,0:T(8,128)} %fusion.56) | copy-start | bytes 12582916 | tf_op jit(solution)/shard_map/while
  310.4 6.0 %copy-start = (f32[1024,1024]{1,0:T(8,128)S(1)}, f32[1024,1024]{1,0:T(8,128)}, u32[]{:S(2)}) copy-start(f32[1024,1024]{1,0:T(8,128)} %fusion.56) | copy-start | bytes 12582916 | tf_op jit(solution)/shard_map/while
  329.5 6.0 %copy-start = (f32[1024,1024]{1,0:T(8,128)S(1)}, f32[1024,1024]{1,0:T(8,128)}, u32[]{:S(2)}) copy-start(f32[1024,1024]{1,0:T(8,128)} %fusion.56) | copy-start | bytes 12582916 | tf_op jit(solution)/shard_map/while
  339.8 96.4 %reduce-scatter.5.cloned.1.call-start = ((), (), s32[]{:S(2)}) async-start(), calls=%async_computation.6 | async-start | bytes 589824 | tf_op jit(solution)/shard_map/reduce_scatter | solution.py:75
Sparse Core Ops, SparseCore 0:
  11.0 59.4 all-gather.8
  73.4 55.2 all-gather.10
  131.7 55.2 all-gather.6
  339.9 30.0 reduce-scatter.2
  373.2 63.0 reduce-scatter.4
